TPU v7x, 128 devices: a whole 4x4x4 slice. The times are simulated.
128 devices in a mesh: ty: 8 (over x, core), tx: 16 (over y, z).
Axes of the slice: x: 4, y: 4, z: 4, core: 2. Of those that a mesh axis runs over, the one named last changes fastest.
Arguments:
- potential_warmth: float32 [16, 1024, 8192], P(None, ('ty', 'tx')), may hold values from -2 to 30
- saltiness_field: float32 [16, 1024, 8192], P(None, ('ty', 'tx')), may hold values from 30 to 38
- ocean_tier_tally: int32 [1024, 8192], P(('ty', 'tx')), may hold values from 0 to 16, as said below
Outputs:
- buoyancy_anomaly: float32 [16, 1024, 8192], P(None, 'ty', 'tx')
- laplacian: float32 [16, 1024, 8192], P(None, 'ty', 'tx')
Inputs may be any that keep to these rules, and one draw needn't show every extreme that they name: `ocean_tier_tally`: columns with 0 are land; the tile of rows 0 .. 127 and columns 0 .. 511 is land in every draw, and other whole tiles of land occur. Within the rows of one device and the columns of one tile, at most 3072 columns are ocean, and some such block has exactly 3072.
All inputs are finite; a program needn't handle non-finite values.
Results may differ from a plain program's by a relative error of at most 0.00002.
Values sent between devices are 32-bit elements; how exact they have to be, the bound alone decides.
A program may use at most 128 MiB of HBM per device.

v0:
```python
import jax
import jax.numpy as jnp
from jax import lax
from jax.experimental import pallas as pl
from jax.experimental.pallas import tpu as pltpu
from jax.sharding import PartitionSpec as P

therm_coef = 0.1655
haline_coef = 0.76554
cabbel_coef = 0.05952
haline_second = 0.00054914
thermo_press = 0.0001497
haline_press = 1.109e-05
cross_coef = 0.0024341

MESH = pl.DeviceIdType.MESH
TIERS = 16
BAND = 8
CJ = 128
CI = 512
NX = 16
NY = 8
COLS = NX * CI
LANES = 128
ROWS = BAND * CI // LANES
KEPT = 24
SPARE = (ROWS - KEPT) * LANES
CUTS = (0, 4, 8, 12, 16)
CHUNKS = len(CUTS) - 1
PAD = BAND
FAR = ((2, 2), (2, 1), (2, 3), (1, 2), (3, 2), (1, 1), (3, 3), (1, 3), (3, 1), (2, 0), (0, 2), (1, 0), (3, 0), (0, 1), (0, 3), (0, 0))
f32 = jnp.float32
i32 = jnp.int32


def density(warmth, salt, tier):
    depth = 5.0 + 10.0 * tier
    a = warmth - 10.0
    b = salt - 35.0
    heat = (-therm_coef * (1.0 + thermo_press * depth)) - (0.5 * therm_coef * cabbel_coef) * a - cross_coef * b
    salty = (haline_coef * (1.0 - haline_press * depth)) - (0.5 * haline_coef * haline_second) * b
    return heat * a + salty * b


def partner_of(tx, step, sign=1):
    dy = jnp.int32(0)
    dz = jnp.int32(0)
    for number, (far_y, far_z) in enumerate(FAR):
        dy = jnp.where(step == number, far_y, dy)
        dz = jnp.where(step == number, far_z, dz)
    if sign < 0:
        dy, dz = 4 - dy, 4 - dz
    return lax.rem(tx // 4 + dy, 4) * 4 + lax.rem(lax.rem(tx, 4) + dz, 4)


def as_rows(block):
    return jnp.concatenate([block[:, LANES * v : LANES * v + LANES] for v in range(CI // LANES)], axis=0)


def as_block(rows):
    return jnp.concatenate([rows[BAND * v : BAND * v + BAND] for v in range(CI // LANES)], axis=1)


def land_counts(land):
    one = lax.broadcasted_iota(i32, (LANES, 2 * LANES), 0)
    two = lax.broadcasted_iota(i32, (LANES, 2 * LANES), 1)
    ahead = jnp.where(jnp.logical_or(two >= LANES, one < two), 1.0, 0.0).astype(jnp.bfloat16)
    both = jnp.dot(land.astype(jnp.bfloat16), ahead, preferred_element_type=f32)
    one = lax.broadcasted_iota(i32, (ROWS, ROWS), 0)
    two = lax.broadcasted_iota(i32, (ROWS, ROWS), 1)
    above = jnp.where(two < one, 1.0, 0.0).astype(jnp.bfloat16)
    start = jnp.dot(above, both[:, LANES:].astype(jnp.bfloat16), preferred_element_type=f32)
    cell = jnp.minimum(start + both[:, :LANES], float(SPARE))
    return jnp.minimum(start, float(SPARE)).astype(i32), cell.astype(i32)


def squeeze(state, bits, axis, roll):
    size = state.shape[axis]
    for bit in range(bits):
        flag = 256 << bit
        ahead = roll(state, size - (1 << bit), axis)
        stay = jnp.where((state & flag) != 0, 0, state)
        state = jnp.where((ahead & flag) != 0, ahead, stay)
    return state


def packing(tally, roll):
    start, cell = land_counts(jnp.where(tally > 0, 0.0, 1.0))
    lane = lax.broadcasted_iota(i32, (ROWS, LANES), 1)
    row = lax.broadcasted_iota(i32, (ROWS, LANES), 0)
    state = jnp.where(tally > 0, ((cell - start) << 8) | 128 | lane, 0)
    state = squeeze(state, 7, 1, roll) & 255
    state = jnp.take_along_axis(state, (lane + start) & 127, axis=1)
    back = (start + lane) >> 7
    rows = jnp.where(state >= 128, (back << 8) | row, 0)
    rows = squeeze(rows, 4, 0, roll) & 31
    return state & 127, rows[:KEPT]


def unpacking(tally):
    start, cell = land_counts(jnp.where(tally > 0, 0.0, 1.0))
    lane = lax.broadcasted_iota(i32, (ROWS, LANES), 1)
    row = lax.broadcasted_iota(i32, (ROWS, LANES), 0)
    return row - ((start + lane) >> 7), (lane - cell) & 127


def pack(rows, lane_from, row_from):
    moved = jnp.take_along_axis(rows, lane_from, axis=1)
    parts = []
    for w in range(KEPT // BAND):
        at = row_from[BAND * w : BAND * w + BAND]
        low = jnp.take_along_axis(moved[BAND * w : BAND * w + BAND], at & 7, axis=0)
        high = jnp.take_along_axis(moved[BAND * w + BAND : BAND * w + 2 * BAND], at & 7, axis=0)
        parts.append(jnp.where(at >= BAND * (w + 1), high, low))
    return jnp.concatenate(parts, axis=0)


def unpack(kept, row_from, lane_from):
    parts = []
    for v in range(ROWS // BAND):
        at = row_from[BAND * v : BAND * v + BAND]
        low = None if v == 0 else jnp.take_along_axis(kept[BAND * v - BAND : BAND * v], at & 7, axis=0)
        high = None if v == KEPT // BAND else jnp.take_along_axis(kept[BAND * v : BAND * v + BAND], at & 7, axis=0)
        if low is None or high is None:
            parts.append(high if low is None else low)
        else:
            parts.append(jnp.where(at >= BAND * v, high, low))
    return jnp.take_along_axis(jnp.concatenate(parts, axis=0), lane_from, axis=1)


def exchange(
    warmth, salt, tally, out, lap,
    heat, brine, bottom, boxes, deeps, depth, least, pack_lane, pack_row, rows_back, rim_low, rim_high, rims, rows_out, rows_in,
    in_sem, send_sem, recv_sem, rim_ssem, rim_rsem, row_ssem, row_rsem,
):
    ty = lax.axis_index("ty")
    tx = lax.axis_index("tx")
    barrier = pltpu.get_barrier_semaphore()
    loads = [pltpu.make_async_copy(tally, bottom, in_sem.at[2 * CHUNKS])]
    for chunk in range(CHUNKS):
        part = pl.ds(CUTS[chunk], CUTS[chunk + 1] - CUTS[chunk])
        loads.append(pltpu.make_async_copy(warmth.at[part], heat.at[part], in_sem.at[2 * chunk]))
        loads.append(pltpu.make_async_copy(salt.at[part], brine.at[part], in_sem.at[2 * chunk + 1]))
    for load in loads:
        load.start()
    for step in range(1, NX):
        pl.semaphore_signal(barrier, inc=1, device_id={"tx": lax.rem(tx + step, NX)}, device_id_type=MESH)

    @pl.when(ty > 0)
    def _():
        pl.semaphore_signal(barrier, inc=1, device_id={"ty": ty - 1}, device_id_type=MESH)

    @pl.when(ty < NY - 1)
    def _():
        pl.semaphore_signal(barrier, inc=1, device_id={"ty": ty + 1}, device_id_type=MESH)

    lanes = lax.broadcasted_iota(i32, (BAND, LANES), 1)

    def levels(chunk):
        return pl.ds(CUTS[chunk], CUTS[chunk + 1] - CUTS[chunk])

    def box_copy(chunk, to, source):
        return pltpu.make_async_remote_copy(
            src_ref=boxes.at[to, levels(chunk)], dst_ref=boxes.at[NX + source, levels(chunk)],
            send_sem=send_sem.at[chunk, to], recv_sem=recv_sem.at[chunk, source],
            device_id={"tx": to}, device_id_type=MESH,
        )

    def deep_copy(to, source):
        return pltpu.make_async_remote_copy(
            src_ref=deeps.at[to], dst_ref=deeps.at[NX + source],
            send_sem=send_sem.at[CHUNKS, to], recv_sem=recv_sem.at[CHUNKS, source],
            device_id={"tx": to}, device_id_type=MESH,
        )

    def rim_copy(to, source):
        return pltpu.make_async_remote_copy(
            src_ref=rim_low.at[to], dst_ref=rims.at[source],
            send_sem=rim_ssem.at[to], recv_sem=rim_rsem.at[source],
            device_id={"tx": to}, device_id_type=MESH,
        )

    def make(chunk, step):
        to = partner_of(tx, step)
        slot = jnp.where(step == NX - 1, NX + to, to)
        east = lax.rem(to + 1, NX)
        west = lax.rem(to + NX - 1, NX)
        at = pl.ds(pl.multiple_of(to * CI, CI), CI)
        low = jnp.zeros((BAND, LANES), f32)
        high = jnp.zeros((BAND, LANES), f32)
        if chunk == 0:
            deep = bottom[:, at]
            lane_from, row_from = packing(as_rows(deep), pltpu.roll)
            pack_lane[to] = lane_from
            pack_row[to] = row_from
            deep = deep.astype(f32)
            deeps[slot] = deep
            low = jnp.where(lanes == TIERS, pltpu.roll(deep[:, CI - LANES :], TIERS + 1, 1), low)
            high = jnp.where(lanes == 32 + TIERS, pltpu.roll(deep[:, :LANES], 32 + TIERS, 1), high)
        else:
            lane_from = pack_lane[to]
            row_from = pack_row[to]
        for tier in range(CUTS[chunk], CUTS[chunk + 1]):
            value = density(heat[tier, :, at], brine[tier, :, at], tier)
            boxes[slot, tier] = pack(as_rows(value), lane_from, row_from)
            low = jnp.where(lanes == tier, pltpu.roll(value[:, CI - LANES :], tier + 1, 1), low)
            high = jnp.where(lanes == 32 + tier, pltpu.roll(value[:, :LANES], 32 + tier, 1), high)
        if chunk == 0:
            rim_low[east] = low
            rim_high[west] = high
        else:
            rim_low[east] = rim_low[east] + low
            rim_high[west] = rim_high[west] + high

    def wait_loads(chunk):
        loads[1 + 2 * chunk].wait()
        loads[2 + 2 * chunk].wait()

    loads[0].wait()
    wait_loads(0)
    make(0, jnp.int32(0))
    neighbours = jnp.where(ty > 0, 1, 0) + jnp.where(ty < NY - 1, 1, 0)
    pl.semaphore_wait(barrier, NX - 1 + neighbours)

    def first_chunk(step, carry):
        make(0, step)
        to = partner_of(tx, step - 1)
        deep_copy(to, tx).start()
        box_copy(0, to, tx).start()
        return carry

    lax.fori_loop(1, NX, first_chunk, 0)
    for chunk in range(1, CHUNKS):
        wait_loads(chunk)

        def later_chunk(step, carry, chunk=chunk):
            make(chunk, step)
            return carry

        lax.fori_loop(0, NX, later_chunk, 0)

    def join(to, carry):
        rim_low[to] = rim_low[to] + rim_high[to]
        return carry

    lax.fori_loop(0, NX, join, 0)
    rims[tx] = rim_low[tx]

    def send_rim(step, carry):
        rim_copy(partner_of(tx, step), tx).start()
        return carry

    lax.fori_loop(0, NX - 1, send_rim, 0)
    for chunk in range(1, CHUNKS):

        def send_chunk(step, carry, chunk=chunk):
            box_copy(chunk, partner_of(tx, step), tx).start()
            return carry

        lax.fori_loop(0, NX - 1, send_chunk, 0)

    def arrive(chunk, source):
        @pl.when(source != tx)
        def _():
            if chunk == 0:
                deep_copy(source, source).wait_recv()
            box_copy(chunk, source, source).wait_recv()

        rows = pl.ds(pl.multiple_of(PAD + source * BAND, BAND), BAND)
        deep = deeps[NX + source]
        if chunk == 0:
            row_from, lane_from = unpacking(as_rows(deep))
            rows_back[source] = row_from
            pack_lane[source] = lane_from
            depth[rows] = deep
        else:
            row_from = rows_back[source]
            lane_from = pack_lane[source]
        for tier in range(CUTS[chunk], CUTS[chunk + 1]):
            value = as_block(unpack(boxes[NX + source, tier], row_from, lane_from))
            out[tier, rows] = jnp.where(deep > tier, value, 0.0)

    def row_copy(chunk, side, device):
        return pltpu.make_async_remote_copy(
            src_ref=rows_out.at[chunk, side], dst_ref=rows_in.at[chunk, 1 - side if device == "ty" else 1],
            send_sem=row_ssem.at[chunk, side], recv_sem=row_rsem.at[chunk, 1 - side if device == "ty" else 1],
            device_id={"ty": jnp.minimum(ty + 1, NY - 1) if side else jnp.maximum(ty - 1, 0)} if device == "ty" else {"tx": NX - 1 - tx},
            device_id_type=MESH,
        )

    def hand_on(chunk):
        @pl.when(ty > 0)
        def _():
            row_copy(chunk, 0, "ty").start()

        @pl.when(ty < NY - 1)
        def _():
            row_copy(chunk, 1, "ty").start()

        @pl.when(ty == NY - 1)
        def _():
            row_copy(chunk, 1, "tx").start()

    def rows_here(chunk):
        @pl.when(ty > 0)
        def _():
            row_copy(chunk, 0, "ty").wait_send()
            row_copy(chunk, 1, "ty").wait_recv()

        @pl.when(ty < NY - 1)
        def _():
            row_copy(chunk, 1, "ty").wait_send()
            row_copy(chunk, 0, "ty").wait_recv()

        @pl.when(ty == NY - 1)
        def _():
            row_copy(chunk, 1, "tx").wait()

        turn = 127 - lanes
        lower = rows_in[chunk, 0]
        upper = rows_in[chunk, 1]
        flipped = [jnp.take_along_axis(upper[:, LANES * v : LANES * v + LANES], turn, axis=1) for v in (3, 2, 1, 0)]
        upper = jnp.where(ty == NY - 1, jnp.concatenate(flipped, axis=1), upper)
        count = CUTS[chunk + 1] - CUTS[chunk]
        for number in range(count):
            out[CUTS[chunk] + number, PAD - 1 : PAD] = lower[number : number + 1]
            out[CUTS[chunk] + number, PAD + CJ : PAD + CJ + 1] = upper[number : number + 1]
        if chunk == 0:
            depth[PAD - 1 : PAD] = jnp.where(ty > 0, lower[count : count + 1], 0.0)
            depth[PAD + CJ : PAD + CJ + 1] = upper[count : count + 1]

    first_row = lax.broadcasted_iota(i32, (BAND, CI), 0) == 0
    last_row = lax.broadcasted_iota(i32, (BAND, CI), 0) == BAND - 1

    def around(ref, band, tier):
        here = ref[PAD + BAND * band : PAD + BAND * band + BAND]
        above = ref[PAD + BAND * band + BAND : PAD + BAND * band + 2 * BAND]
        below = ref[PAD + BAND * band - BAND : PAD + BAND * band]
        north = jnp.where(last_row, pltpu.roll(above, BAND - 1, 0), pltpu.roll(here, BAND - 1, 0))
        south = jnp.where(first_row, pltpu.roll(below, 1, 0), pltpu.roll(here, 1, 0))
        rim = rims[band]
        east = pltpu.roll(here, CI - 1, 1)
        east_rim = pltpu.roll(rim, (127 - 32 - tier + LANES) % LANES if isinstance(tier, int) else 127 - 32 - tier, 1)
        east = jnp.concatenate([east[:, : CI - LANES], jnp.where(lanes == 127, east_rim, east[:, CI - LANES :])], 1)
        west = pltpu.roll(here, 1, 1)
        west = jnp.concatenate([jnp.where(lanes == 0, pltpu.roll(rim, LANES - tier, 1), west[:, :LANES]), west[:, LANES:]], 1)
        return here, north, south, east, west

    def bounds(band):
        here, *others = around(depth, band, TIERS)
        for side, other in enumerate(others):
            least[side, BAND * band : BAND * band + BAND] = jnp.minimum(here, other)

    def laplace(chunk, bands):
        def one(tier, carry):
            level = tier.astype(f32)
            field = out.at[tier]
            for band in bands:
                here, *others = around(field, band, tier)
                total = None
                for side, other in enumerate(others):
                    term = jnp.where(least[side, BAND * band : BAND * band + BAND] > level, other - here, 0.0)
                    total = term if total is None else total + term
                lap[tier, BAND * band : BAND * band + BAND] = total
            return carry

        lax.fori_loop(CUTS[chunk], CUTS[chunk + 1], one, 0)

    inner = list(range(1, NX - 1))
    for chunk in range(CHUNKS):
        arrive(chunk, 0)
        arrive(chunk, NX - 1)
        count = CUTS[chunk + 1] - CUTS[chunk]
        for number in range(count):
            tier = CUTS[chunk] + number
            rows_out[chunk, 0, number : number + 1] = out[tier, PAD : PAD + 1]
            rows_out[chunk, 1, number : number + 1] = out[tier, PAD + CJ - 1 : PAD + CJ]
        if chunk == 0:
            rows_out[chunk, 0, count : count + 1] = depth[PAD : PAD + 1]
            rows_out[chunk, 1, count : count + 1] = depth[PAD + CJ - 1 : PAD + CJ]
        arrive(chunk, 1)
        hand_on(chunk)

        def rest(source, carry, chunk=chunk):
            arrive(chunk, source)
            return carry

        lax.fori_loop(2, NX - 1, rest, 0)
        if chunk == 0:

            def rim_in(source, carry):
                @pl.when(source != tx)
                def _():
                    rim_copy(source, source).wait_recv()

                return carry

            lax.fori_loop(0, NX, rim_in, 0)
            for band in inner:
                bounds(band)
        laplace(chunk, inner)
        rows_here(chunk)
        if chunk == 0:
            bounds(0)
            bounds(NX - 1)
        laplace(chunk, (0, NX - 1))

    def sent(to, carry):
        @pl.when(to != tx)
        def _():
            deep_copy(to, tx).wait_send()
            rim_copy(to, tx).wait_send()
            for chunk in range(CHUNKS):
                box_copy(chunk, to, tx).wait_send()

        return carry

    lax.fori_loop(0, NX, sent, 0)


def write_out(field, lap, field_out, lap_out, sem):
    copies = []
    for part in range(4):
        at = pl.ds(part * TIERS // 4, TIERS // 4)
        copies.append(pltpu.make_async_copy(field.at[at, PAD : PAD + CJ], field_out.at[at], sem.at[2 * part]))
        copies.append(pltpu.make_async_copy(lap.at[at], lap_out.at[at], sem.at[2 * part + 1]))
    for copy in copies:
        copy.start()
    for copy in copies:
        copy.wait()


def on_device(warmth, salt, tally):
    hbm = pl.BlockSpec(memory_space=pltpu.HBM)
    vmem = pl.BlockSpec(memory_space=pltpu.VMEM)
    field, lap = pl.pallas_call(
        exchange,
        out_shape=(pltpu.VMEM((TIERS, CJ + 2 * PAD, CI), f32), pltpu.VMEM((TIERS, CJ, CI), f32)),
        in_specs=[hbm] * 3,
        out_specs=(vmem,) * 2,
        scratch_shapes=[
            pltpu.VMEM((TIERS, BAND, COLS), f32),
            pltpu.VMEM((TIERS, BAND, COLS), f32),
            pltpu.VMEM((BAND, COLS), i32),
            pltpu.VMEM((2 * NX, TIERS, KEPT, LANES), f32),
            pltpu.VMEM((2 * NX, BAND, CI), f32),
            pltpu.VMEM((CJ + 2 * PAD, CI), f32),
            pltpu.VMEM((4, CJ, CI), f32),
            pltpu.VMEM((NX, ROWS, LANES), i32),
            pltpu.VMEM((NX, KEPT, LANES), i32),
            pltpu.VMEM((NX, ROWS, LANES), i32),
            pltpu.VMEM((NX, BAND, LANES), f32),
            pltpu.VMEM((NX, BAND, LANES), f32),
            pltpu.VMEM((NX, BAND, LANES), f32),
            pltpu.VMEM((CHUNKS, 2, BAND, CI), f32),
            pltpu.VMEM((CHUNKS, 2, BAND, CI), f32),
            pltpu.SemaphoreType.DMA((2 * CHUNKS + 1,)),
            pltpu.SemaphoreType.DMA((CHUNKS + 1, NX)),
            pltpu.SemaphoreType.DMA((CHUNKS + 1, NX)),
            pltpu.SemaphoreType.DMA((NX,)),
            pltpu.SemaphoreType.DMA((NX,)),
            pltpu.SemaphoreType.DMA((CHUNKS, 2)),
            pltpu.SemaphoreType.DMA((CHUNKS, 2)),
        ],
        compiler_params=pltpu.CompilerParams(collective_id=0, has_side_effects=True, vmem_limit_bytes=40 * 2**20),
        name="exchange",
    )(warmth, salt, tally)
    return pl.pallas_call(
        write_out,
        out_shape=(jax.ShapeDtypeStruct((TIERS, CJ, CI), f32),) * 2,
        in_specs=[pl.BlockSpec(memory_space=pl.ANY)] * 2,
        out_specs=(hbm,) * 2,
        scratch_shapes=[pltpu.SemaphoreType.DMA((8,))],
        compiler_params=pltpu.CompilerParams(vmem_limit_bytes=16 * 2**20),
        name="write_out",
    )(field, lap)


def solution(mesh):
    placed = (P(None, ("ty", "tx"), None), P(None, ("ty", "tx"), None), P(("ty", "tx"), None))
    return jax.shard_map(
        on_device,
        mesh=mesh,
        in_specs=placed,
        out_specs=(P(None, "ty", "tx"), P(None, "ty", "tx")),
        check_vma=False,
    )
```

profile of v0, /device:TPU:7, one launch (start us, length us, event | category | flops | bytes accessed | tf_op | source)
XLA Modules:
  0.0 79.7 jit_solution(17618119949033709149)
XLA Ops:
  0.6 0.0 copy-start
  0.6 2.2 %copy-done = f32[16,8,8192]{2,1,0:T(8,128)S(1)} copy-done((f32[16,8,8192]{2,1,0:T(8,128)S(1)}, f32[16,8,8192]{2,1,0:T(8,128)}, u32[]{:S(2)}) %copy-start) | copy-done | bytes 4194328
  2.8 0.0 copy-start.1
  2.8 0.9 %copy-done.1 = s32[8,8192]{1,0:T(8,128)S(1)} copy-done((s32[8,8192]{1,0:T(8,128)S(1)}, s32[8,8192]{1,0:T(8,128)}, u32[]{:S(2)}) %copy-start.1) | copy-done | bytes 262168
  3.8 72.5 %exchange.1 = (f32[16,144,512]{2,1,0:T(8,128)S(1)}, f32[16,128,512]{2,1,0:T(8,128)S(1)}) custom-call(f32[16,8,8192]{2,1,0:T(8,128)S(1)} %copy-done, f32[16,8,8192]{2,1,0:T(8,128)} %salt.1, s32[8,8192]{1,0:T(8,128)S(1)} %copy-done.1), custom_call_target="tpu_custom_call" | custom-call | tf_op jit(solution)/shard_map/exchange/pallas_call | solution.py:436
  76.3 3.4 %write_out.1 = (f32[16,128,512]{2,1,0:T(8,128)}, f32[16,128,512]{2,1,0:T(8,128)}) custom-call(f32[16,144,512]{2,1,0:T(8,128)S(1)} %get-tuple-element.4.field, f32[16,128,512]{2,1,0:T(8,128)S(1)} %get-tuple-element.5.lap), custom_call_target="tpu_custom_call" | custom-call | tf_op jit(solution)/shard_map/write_out/pallas_call | solution.py:468
Async XLA Ops:
  0.6 2.2 %copy-start = (f32[16,8,8192]{2,1,0:T(8,128)S(1)}, f32[16,8,8192]{2,1,0:T(8,128)}, u32[]{:S(2)}) copy-start(f32[16,8,8192]{2,1,0:T(8,128)} %warmth.1) | copy-start | bytes 12582916
  2.8 0.9 %copy-start.1 = (s32[8,8192]{1,0:T(8,128)S(1)}, s32[8,8192]{1,0:T(8,128)}, u32[]{:S(2)}) copy-start(s32[8,8192]{1,0:T(8,128)} %tally.1) | copy-start | bytes 786436
where the time goes:
time: 79.9 us; the launch traced here: 79.7 us
  Pallas kernels  75.9 us (95%)
  local copies, waits for them, and re-layouts  3.13 us (4%)
    pallas_call x1, Pallas kernels, on_device(): pl.pallas_call(exchange, out_shape=(pltpu.VMEM((TIERS, CJ + 2 * PAD, CI),...  72.5 us
    pallas_call x1, Pallas kernels, on_device(): pl.pallas_call(write_out, out_shape=(jax.ShapeDtypeStruct((TIERS, CJ, CI)...  3.37 us
    unnamed x4, local copies, waits for them, and re-layouts  3.13 us

commit v1 on v0

--- a/solution.py
+++ b/solution.py
@@ -42,15 +42,13 @@
     return heat * a + salty * b
 
 
-def partner_of(tx, step, sign=1):
+def partner_of(tx, step):
     dy = jnp.int32(0)
     dz = jnp.int32(0)
     for number, (far_y, far_z) in enumerate(FAR):
         dy = jnp.where(step == number, far_y, dy)
         dz = jnp.where(step == number, far_z, dz)
-    if sign < 0:
-        dy, dz = 4 - dy, 4 - dz
-    return lax.rem(tx // 4 + dy, 4) * 4 + lax.rem(lax.rem(tx, 4) + dz, 4)
+    return ((tx // 4 + dy) & 3) * 4 + ((tx + dz) & 3)
 
 
 def as_rows(block):
@@ -246,18 +244,12 @@
     lax.fori_loop(0, NX, join, 0)
     rims[tx] = rim_low[tx]
 
-    def send_rim(step, carry):
-        rim_copy(partner_of(tx, step), tx).start()
-        return carry
-
-    lax.fori_loop(0, NX - 1, send_rim, 0)
+    partners = [((tx // 4 + dy) & 3) * 4 + ((tx + dz) & 3) for dy, dz in FAR[:-1]]
+    for to in partners:
+        rim_copy(to, tx).start()
     for chunk in range(1, CHUNKS):
-
-        def send_chunk(step, carry, chunk=chunk):
-            box_copy(chunk, partner_of(tx, step), tx).start()
-            return carry
-
-        lax.fori_loop(0, NX - 1, send_chunk, 0)
+        for to in partners:
+            box_copy(chunk, to, tx).start()
 
     def arrive(chunk, source):
         @pl.when(source != tx)
@@ -351,7 +343,7 @@
         for side, other in enumerate(others):
             least[side, BAND * band : BAND * band + BAND] = jnp.minimum(here, other)
 
-    def laplace(chunk, bands):
+    def laplace(chunk, bands, stop=None):
         def one(tier, carry):
             level = tier.astype(f32)
             field = out.at[tier]
@@ -364,7 +356,7 @@
                 lap[tier, BAND * band : BAND * band + BAND] = total
             return carry
 
-        lax.fori_loop(CUTS[chunk], CUTS[chunk + 1], one, 0)
+        lax.fori_loop(CUTS[chunk], CUTS[chunk + 1] if stop is None else stop, one, 0)
 
     inner = list(range(1, NX - 1))
     for chunk in range(CHUNKS):
@@ -399,11 +391,12 @@
             for band in inner:
                 bounds(band)
         laplace(chunk, inner)
+
+    for chunk in range(CHUNKS):
         rows_here(chunk)
-        if chunk == 0:
-            bounds(0)
-            bounds(NX - 1)
-        laplace(chunk, (0, NX - 1))
+    bounds(0)
+    bounds(NX - 1)
+    laplace(0, (0, NX - 1), TIERS)
 
     def sent(to, carry):
         @pl.when(to != tx)
@@ -462,7 +455,7 @@
             pltpu.SemaphoreType.DMA((CHUNKS, 2)),
             pltpu.SemaphoreType.DMA((CHUNKS, 2)),
         ],
-        compiler_params=pltpu.CompilerParams(collective_id=0, has_side_effects=True, vmem_limit_bytes=40 * 2**20),
+        compiler_params=pltpu.CompilerParams(collective_id=0, has_side_effects=True, vmem_limit_bytes=50 * 2**20),
         name="exchange",
     )(warmth, salt, tally)
     return pl.pallas_call(

time: 79.9 us -> 66.6 us (0.83); the launches traced: 79.7 us -> 65.5 us
  Pallas kernels: 75.9 us -> 64.9 us
  local copies, waits for them, and re-layouts: 3.13 us -> 0 us
    pallas_call x1, Pallas kernels: 72.5 us -> 61.5 us  [on_device(): pl.pallas_call(exchange, out_shape=(pltpu.VMEM((TIERS, CJ + 2 * PAD, CI),...]
    unnamed x4 -> x0, local copies, waits for them, and re-layouts: 3.13 us -> none
where the time goes in v1:
time: 66.6 us; the launch traced here: 65.5 us
  Pallas kernels  64.9 us (97%)
    pallas_call x1, Pallas kernels, on_device(): pl.pallas_call(exchange, out_shape=(pltpu.VMEM((TIERS, CJ + 2 * PAD, CI),...  61.5 us
    pallas_call x1, Pallas kernels, on_device(): pl.pallas_call(write_out, out_shape=(jax.ShapeDtypeStruct((TIERS, CJ, CI)...  3.37 us

profile of v1, /device:TPU:7, one launch (start us, length us, event | category | flops | bytes accessed | tf_op | source)
XLA Modules:
  0.0 65.5 jit_solution(15466108928547837600)
XLA Ops:
  0.6 61.5 %exchange.1 = (f32[16,144,512]{2,1,0:T(8,128)S(1)}, f32[16,128,512]{2,1,0:T(8,128)S(1)}) custom-call(f32[16,8,8192]{2,1,0:T(8,128)} %warmth.1, f32[16,8,8192]{2,1,0:T(8,128)} %salt.1, s32[8,8192]{1,0:T(8,128)} %tally.1), custom_call_target="tpu_custom_call" | custom-call | tf_op jit(solution)/shard_map/exchange/pallas_call | solution.py:429
  62.2 3.4 %write_out.1 = (f32[16,128,512]{2,1,0:T(8,128)}, f32[16,128,512]{2,1,0:T(8,128)}) custom-call(f32[16,144,512]{2,1,0:T(8,128)S(1)} %get-tuple-element.4.field, f32[16,128,512]{2,1,0:T(8,128)S(1)} %get-tuple-element.5.lap), custom_call_target="tpu_custom_call" | custom-call | tf_op jit(solution)/shard_map/write_out/pallas_call | solution.py:461

commit v2 on v1

v2 whole, which is shorter than its diff:
```python
import jax
import jax.numpy as jnp
from jax import lax
from jax.experimental import pallas as pl
from jax.experimental.pallas import tpu as pltpu
from jax.sharding import PartitionSpec as P

therm_coef = 0.1655
haline_coef = 0.76554
cabbel_coef = 0.05952
haline_second = 0.00054914
thermo_press = 0.0001497
haline_press = 1.109e-05
cross_coef = 0.0024341

MESH = pl.DeviceIdType.MESH
TIERS = 16
BAND = 8
CJ = 128
CI = 512
NX = 16
NY = 8
COLS = NX * CI
LANES = 128
ROWS = BAND * CI // LANES
KEPT = 24
SPARE = (ROWS - KEPT) * LANES
CUTS = (0, 5, 10, 14, 16)
CHUNKS = len(CUTS) - 1
EARLY = CUTS[-2]
BOX = ROWS + TIERS * KEPT
INNER = range(1, NX - 1)
LAST = NX - 1
FAR = ((2, 2), (2, 1), (2, 3), (1, 2), (3, 2), (1, 1), (3, 3), (1, 3), (3, 1), (2, 0), (0, 2), (1, 0), (3, 0), (0, 1), (0, 3), (0, 0))
f32 = jnp.float32
i32 = jnp.int32


def density(warmth, salt, tier):
    depth = 5.0 + 10.0 * tier
    a = warmth - 10.0
    b = salt - 35.0
    heat = (-therm_coef * (1.0 + thermo_press * depth)) - (0.5 * therm_coef * cabbel_coef) * a - cross_coef * b
    salty = (haline_coef * (1.0 - haline_press * depth)) - (0.5 * haline_coef * haline_second) * b
    return heat * a + salty * b


def partner_of(tx, step):
    dy = jnp.int32(0)
    dz = jnp.int32(0)
    for number, (far_y, far_z) in enumerate(FAR):
        dy = jnp.where(step == number, far_y, dy)
        dz = jnp.where(step == number, far_z, dz)
    return ((tx // 4 + dy) & 3) * 4 + ((tx + dz) & 3)


def as_rows(block):
    return jnp.concatenate([block[:, LANES * v : LANES * v + LANES] for v in range(CI // LANES)], axis=0)


def as_block(rows):
    return jnp.concatenate([rows[BAND * v : BAND * v + BAND] for v in range(CI // LANES)], axis=1)


def land_counts(land):
    one = lax.broadcasted_iota(i32, (LANES, 2 * LANES), 0)
    two = lax.broadcasted_iota(i32, (LANES, 2 * LANES), 1)
    ahead = jnp.where(jnp.logical_or(two >= LANES, one < two), 1.0, 0.0).astype(jnp.bfloat16)
    both = jnp.dot(land.astype(jnp.bfloat16), ahead, preferred_element_type=f32)
    one = lax.broadcasted_iota(i32, (ROWS, ROWS), 0)
    two = lax.broadcasted_iota(i32, (ROWS, ROWS), 1)
    above = jnp.where(two < one, 1.0, 0.0).astype(jnp.bfloat16)
    start = jnp.dot(above, both[:, LANES:].astype(jnp.bfloat16), preferred_element_type=f32)
    cell = jnp.minimum(start + both[:, :LANES], float(SPARE))
    return jnp.minimum(start, float(SPARE)).astype(i32), cell.astype(i32)


def squeeze(state, bits, axis, roll):
    size = state.shape[axis]
    for bit in range(bits):
        flag = 256 << bit
        ahead = roll(state, size - (1 << bit), axis)
        stay = jnp.where((state & flag) != 0, 0, state)
        state = jnp.where((ahead & flag) != 0, ahead, stay)
    return state


def packing(tally, roll):
    start, cell = land_counts(jnp.where(tally > 0, 0.0, 1.0))
    lane = lax.broadcasted_iota(i32, (ROWS, LANES), 1)
    row = lax.broadcasted_iota(i32, (ROWS, LANES), 0)
    state = jnp.where(tally > 0, ((cell - start) << 8) | 128 | lane, 0)
    state = squeeze(state, 7, 1, roll) & 255
    state = jnp.take_along_axis(state, (lane + start) & 127, axis=1)
    back = (start + lane) >> 7
    rows = jnp.where(state >= 128, (back << 8) | row, 0)
    rows = squeeze(rows, 4, 0, roll) & 31
    return state & 127, rows[:KEPT]


def unpacking(tally):
    start, cell = land_counts(jnp.where(tally > 0, 0.0, 1.0))
    lane = lax.broadcasted_iota(i32, (ROWS, LANES), 1)
    row = lax.broadcasted_iota(i32, (ROWS, LANES), 0)
    return row - ((start + lane) >> 7), (lane - cell) & 127


def pack(rows, lane_from, row_from):
    moved = jnp.take_along_axis(rows, lane_from, axis=1)
    parts = []
    for w in range(KEPT // BAND):
        at = row_from[BAND * w : BAND * w + BAND]
        low = jnp.take_along_axis(moved[BAND * w : BAND * w + BAND], at & 7, axis=0)
        high = jnp.take_along_axis(moved[BAND * w + BAND : BAND * w + 2 * BAND], at & 7, axis=0)
        parts.append(jnp.where(at >= BAND * (w + 1), high, low))
    return jnp.concatenate(parts, axis=0)


def unpack(kept, row_from, lane_from):
    parts = []
    for v in range(ROWS // BAND):
        at = row_from[BAND * v : BAND * v + BAND]
        low = None if v == 0 else jnp.take_along_axis(kept[BAND * v - BAND : BAND * v], at & 7, axis=0)
        high = None if v == KEPT // BAND else jnp.take_along_axis(kept[BAND * v : BAND * v + BAND], at & 7, axis=0)
        if low is None or high is None:
            parts.append(high if low is None else low)
        else:
            parts.append(jnp.where(at >= BAND * v, high, low))
    return jnp.take_along_axis(jnp.concatenate(parts, axis=0), lane_from, axis=1)


def around(ref, band, tier, rims, above=None, below=None):
    lanes = lax.broadcasted_iota(i32, (BAND, LANES), 1)
    row = lax.broadcasted_iota(i32, (BAND, CI), 0)
    here = ref[BAND * band : BAND * band + BAND]
    if above is None:
        above = pltpu.roll(ref[BAND * band + BAND : BAND * band + 2 * BAND], BAND - 1, 0)
    if below is None:
        below = pltpu.roll(ref[BAND * band - BAND : BAND * band], 1, 0)
    north = jnp.where(row == BAND - 1, above, pltpu.roll(here, BAND - 1, 0))
    south = jnp.where(row == 0, below, pltpu.roll(here, 1, 0))
    rim = rims[band]
    east = pltpu.roll(here, CI - 1, 1)
    east_rim = pltpu.roll(rim, 127 - 32 - tier, 1)
    east = jnp.concatenate([east[:, : CI - LANES], jnp.where(lanes == 127, east_rim, east[:, CI - LANES :])], 1)
    west = pltpu.roll(here, 1, 1)
    west_rim = pltpu.roll(rim, LANES - tier, 1)
    west = jnp.concatenate([jnp.where(lanes == 0, west_rim, west[:, :LANES]), west[:, LANES:]], 1)
    return here, north, south, east, west


def divergence(cells, bounds, level):
    here, *others = cells
    total = None
    for bound, other in zip(bounds, others):
        term = jnp.where(bound > level, other - here, 0.0)
        total = term if total is None else total + term
    return total


def exchange(
    warmth, salt, tally, out, lap, depth, least, rims, edges,
    heat, brine, bottom, boxes, pack_lane, pack_row, lane_back, row_back, rim_low, rim_high, brink_out, brink_in, rows_out, rows_in,
    in_sem, send_sem, recv_sem, rim_ssem, rim_rsem, brink_ssem, brink_rsem, row_ssem, row_rsem,
):
    ty = lax.axis_index("ty")
    tx = lax.axis_index("tx")
    outer = jnp.logical_or(tx == 0, tx == LAST)
    barrier = pltpu.get_barrier_semaphore()
    loads = [pltpu.make_async_copy(tally, bottom, in_sem.at[2 * CHUNKS])]
    for chunk in range(CHUNKS):
        part = pl.ds(CUTS[chunk], CUTS[chunk + 1] - CUTS[chunk])
        loads.append(pltpu.make_async_copy(warmth.at[part], heat.at[part], in_sem.at[2 * chunk]))
        loads.append(pltpu.make_async_copy(salt.at[part], brine.at[part], in_sem.at[2 * chunk + 1]))
    for step in range(1, NX):
        pl.semaphore_signal(barrier, inc=1, device_id={"tx": (tx + step) & LAST}, device_id_type=MESH)

    @pl.when(ty > 0)
    def _():
        pl.semaphore_signal(barrier, inc=1, device_id={"ty": ty - 1}, device_id_type=MESH)

    @pl.when(ty < NY - 1)
    def _():
        pl.semaphore_signal(barrier, inc=1, device_id={"ty": ty + 1}, device_id_type=MESH)

    for load in loads:
        load.start()
    lanes = lax.broadcasted_iota(i32, (BAND, LANES), 1)
    partners = [((tx // 4 + dy) & 3) * 4 + ((tx + dz) & 3) for dy, dz in FAR[:-1]]

    def box_copy(chunk, to, source):
        low = 0 if chunk == 0 else ROWS + KEPT * CUTS[chunk]
        part = pl.ds(low, ROWS + KEPT * CUTS[chunk + 1] - low)
        return pltpu.make_async_remote_copy(
            src_ref=boxes.at[to, part], dst_ref=boxes.at[NX + source, part],
            send_sem=send_sem.at[chunk, to], recv_sem=recv_sem.at[chunk, source],
            device_id={"tx": to}, device_id_type=MESH,
        )

    def rim_copy(to, source):
        return pltpu.make_async_remote_copy(
            src_ref=rim_low.at[to], dst_ref=rims.at[source],
            send_sem=rim_ssem.at[to], recv_sem=rim_rsem.at[source],
            device_id={"tx": to}, device_id_type=MESH,
        )

    def brink_copy(to, source):
        side = jnp.where(source == 0, 0, 1)
        return pltpu.make_async_remote_copy(
            src_ref=brink_out.at[to], dst_ref=brink_in.at[side],
            send_sem=brink_ssem.at[to], recv_sem=brink_rsem.at[side],
            device_id={"tx": to}, device_id_type=MESH,
        )

    def make(first, last, step):
        to = partner_of(tx, step)
        slot = jnp.where(step == LAST, NX + to, to)
        east = (to + 1) & LAST
        west = (to + LAST) & LAST
        at = pl.ds(pl.multiple_of(to * CI, CI), CI)
        low = jnp.zeros((BAND, LANES), f32)
        high = jnp.zeros((BAND, LANES), f32)
        if first == 0:
            deep = bottom[:, at]
            lane_from, row_from = packing(as_rows(deep), pltpu.roll)
            pack_lane[to] = lane_from
            pack_row[to] = row_from
            deep = deep.astype(f32)
            boxes[slot, :ROWS] = as_rows(deep)
            low = jnp.where(lanes == TIERS, pltpu.roll(deep[:, CI - LANES :], TIERS + 1, 1), low)
            high = jnp.where(lanes == 32 + TIERS, pltpu.roll(deep[:, :LANES], 32 + TIERS, 1), high)
        else:
            lane_from = pack_lane[to]
            row_from = pack_row[to]
        for tier in range(first, last):
            value = density(heat[tier, :, at], brine[tier, :, at], tier)
            boxes[slot, ROWS + KEPT * tier : ROWS + KEPT * tier + KEPT] = pack(as_rows(value), lane_from, row_from)
            low = jnp.where(lanes == tier, pltpu.roll(value[:, CI - LANES :], tier + 1, 1), low)
            high = jnp.where(lanes == 32 + tier, pltpu.roll(value[:, :LANES], 32 + tier, 1), high)
            if tier >= EARLY:
                brink = jnp.where(tx == 0, value[:1], value[BAND - 1 :])
                for v in range(CI // LANES):
                    place = (tier - EARLY) * (CI // LANES) + v
                    brink_out[to, place : place + 1] = brink[:, LANES * v : LANES * v + LANES]
        if first == 0:
            rim_low[east] = low
            rim_high[west] = high
        else:
            rim_low[east] = rim_low[east] + low
            rim_high[west] = rim_high[west] + high

    def wait_loads(chunk):
        loads[1 + 2 * chunk].wait()
        loads[2 + 2 * chunk].wait()

    def make_only(first, last):
        def one(step, carry):
            make(first, last, step)
            return carry

        return one

    def make_and_send(chunk):
        def one(step, carry):
            make(CUTS[chunk], CUTS[chunk + 1], step)

            @pl.when(step > 0)
            def _():
                box_copy(chunk, partner_of(tx, step - 1), tx).start()

            return carry

        return one

    loads[0].wait()
    wait_loads(0)
    lax.fori_loop(0, 3, make_only(CUTS[0], CUTS[1]), 0)
    neighbours = jnp.where(ty > 0, 1, 0) + jnp.where(ty < NY - 1, 1, 0)
    pl.semaphore_wait(barrier, NX - 1 + neighbours)
    for to in partners[:2]:
        box_copy(0, to, tx).start()
    lax.fori_loop(3, NX, make_and_send(0), 0)
    wait_loads(1)
    lax.fori_loop(0, NX, make_and_send(1), 0)
    wait_loads(2)
    wait_loads(3)
    lax.fori_loop(0, NX, make_only(CUTS[2], CUTS[4]), 0)

    def join(to, carry):
        rim_low[to] = rim_low[to] + rim_high[to]
        return carry

    lax.fori_loop(0, NX, join, 0)
    rims[tx] = rim_low[tx]

    @pl.when(outer)
    def _():
        brink_in[jnp.where(tx == 0, 0, 1)] = brink_out[tx]
        for to in partners:
            brink_copy(to, tx).start()

    for to in partners:
        rim_copy(to, tx).start()
    for chunk in (2, 3):
        for to in partners:
            box_copy(chunk, to, tx).start()

    def arrive(chunk, source):
        @pl.when(source != tx)
        def _():
            box_copy(chunk, source, source).wait_recv()

        rows = pl.ds(pl.multiple_of(source * BAND, BAND), BAND)
        deep = boxes[NX + source, :ROWS]
        if chunk == 0:
            row_from, lane_from = unpacking(deep)
            row_back[source] = row_from
            lane_back[source] = lane_from
            deep = as_block(deep)
            depth[rows] = deep
        else:
            row_from = row_back[source]
            lane_from = lane_back[source]
            deep = as_block(deep)
        for tier in range(CUTS[chunk], CUTS[chunk + 1]):
            kept = boxes[NX + source, ROWS + KEPT * tier : ROWS + KEPT * tier + KEPT]
            out[tier, rows] = jnp.where(deep > tier, as_block(unpack(kept, row_from, lane_from)), 0.0)

    def arrive_all(chunk, first=0, last=NX):
        def one(source, carry):
            arrive(chunk, source)
            return carry

        lax.fori_loop(first, last, one, 0)

    def laplace(chunk):
        def one(tier, carry):
            for band in INNER:
                rows = slice(BAND * band, BAND * band + BAND)
                bounds = [least[side, rows] for side in range(4)]
                lap[tier, rows] = divergence(around(out.at[tier], band, tier, rims), bounds, tier.astype(f32))
            return carry

        lax.fori_loop(CUTS[chunk], CUTS[chunk + 1], one, 0)

    arrive_all(0)
    arrive_all(1)

    def rim_in(source, carry):
        @pl.when(source != tx)
        def _():
            rim_copy(source, source).wait_recv()

        return carry

    lax.fori_loop(0, NX, rim_in, 0)
    for band in INNER:
        here, *others = around(depth, band, TIERS, rims)
        for side, other in enumerate(others):
            least[side, BAND * band : BAND * band + BAND] = jnp.minimum(here, other)
    laplace(0)
    laplace(1)

    arrive(2, 0)
    arrive(2, LAST)
    for side, at in ((0, 0), (1, CJ - 1)):
        @pl.when(tx != (LAST if side else 0))
        def _():
            brink_copy(LAST if side else 0, LAST if side else 0).wait_recv()

        for tier in range(EARLY):
            rows_out[side, tier : tier + 1] = out[tier, at : at + 1]
        rows_out[side, TIERS : TIERS + 1] = depth[at : at + 1]
        for place in range((TIERS - EARLY) * CI // LANES):
            tier, v = EARLY + place // (CI // LANES), place % (CI // LANES)
            rows_out[side, tier : tier + 1, LANES * v : LANES * v + LANES] = brink_in[side, place : place + 1]

    arrive(2, 1)

    def row_copy(side, along):
        place = 1 - side if along == "ty" else 1
        if along == "ty":
            device = {"ty": jnp.minimum(ty + 1, NY - 1) if side else jnp.maximum(ty - 1, 0)}
        else:
            device = {"tx": LAST - tx}
        return pltpu.make_async_remote_copy(
            src_ref=rows_out.at[side], dst_ref=rows_in.at[place], send_sem=row_ssem.at[side], recv_sem=row_rsem.at[place],
            device_id=device, device_id_type=MESH,
        )

    @pl.when(ty > 0)
    def _():
        row_copy(0, "ty").start()

    @pl.when(ty < NY - 1)
    def _():
        row_copy(1, "ty").start()

    @pl.when(ty == NY - 1)
    def _():
        row_copy(1, "tx").start()

    arrive_all(2, 2, LAST)
    laplace(2)
    arrive_all(3)

    @pl.when(ty > 0)
    def _():
        row_copy(0, "ty").wait_send()
        row_copy(1, "ty").wait_recv()

    @pl.when(ty < NY - 1)
    def _():
        row_copy(1, "ty").wait_send()
        row_copy(0, "ty").wait_recv()

    @pl.when(ty == NY - 1)
    def _():
        row_copy(1, "tx").wait()

    edges[0] = rows_in[0]
    edges[0, TIERS : TIERS + 1] = jnp.where(ty > 0, rows_in[0, TIERS : TIERS + 1], 0.0)
    turn = 127 - lax.broadcasted_iota(i32, (24, LANES), 1)
    upper = rows_in[1]
    flipped = [jnp.take_along_axis(upper[:, LANES * v : LANES * v + LANES], turn, axis=1) for v in (3, 2, 1, 0)]
    edges[1] = jnp.where(ty == NY - 1, jnp.concatenate(flipped, axis=1), upper)

    @pl.when(outer)
    def _():
        for to in partners:
            brink_copy(to, tx).wait_send()

    for to in partners:
        rim_copy(to, tx).wait_send()
        for chunk in range(CHUNKS):
            box_copy(chunk, to, tx).wait_send()


def finish(field, lap, depth, least, rims, edges, field_out, lap_out, ends, late, sem):
    middle = pl.ds(BAND, CJ - 2 * BAND)
    half = TIERS // 2
    copies = [pltpu.make_async_copy(field.at[pl.ds(half * n, half)], field_out.at[pl.ds(half * n, half)], sem.at[n]) for n in (0, 1)]
    copies.append(pltpu.make_async_copy(lap.at[pl.ds(0, EARLY), middle], lap_out.at[pl.ds(0, EARLY), middle], sem.at[2]))
    for copy in copies:
        copy.start()

    def outer(ref, tier, band):
        row = edges[1 if band else 0, tier : tier + 1]
        return around(ref, band, tier, rims, **{"above" if band else "below": row})

    for place, band in enumerate((0, LAST)):
        here, *others = outer(depth, TIERS, band)
        bounds = [jnp.minimum(here, other) for other in others]
        for tier in range(TIERS):
            ends[place, tier] = divergence(outer(field.at[tier], tier, band), bounds, tier)
        copies.append(pltpu.make_async_copy(ends.at[place], lap_out.at[:, pl.ds(BAND * band, BAND)], sem.at[3 + place]))
        copies[-1].start()
    for tier in range(EARLY, TIERS):
        for band in INNER:
            bounds = [least[side, BAND * band : BAND * band + BAND] for side in range(4)]
            late[tier - EARLY, BAND * (band - 1) : BAND * band] = divergence(around(field.at[tier], band, tier, rims), bounds, tier)
    copies.append(pltpu.make_async_copy(late, lap_out.at[pl.ds(EARLY, TIERS - EARLY), middle], sem.at[5]))
    copies[-1].start()
    for copy in copies:
        copy.wait()


def on_device(warmth, salt, tally):
    hbm = pl.BlockSpec(memory_space=pltpu.HBM)
    vmem = pl.BlockSpec(memory_space=pltpu.VMEM)
    held = pl.pallas_call(
        exchange,
        out_shape=(
            pltpu.VMEM((TIERS, CJ, CI), f32),
            pltpu.VMEM((TIERS, CJ, CI), f32),
            pltpu.VMEM((CJ, CI), f32),
            pltpu.VMEM((4, CJ, CI), f32),
            pltpu.VMEM((NX, BAND, LANES), f32),
            pltpu.VMEM((2, 24, CI), f32),
        ),
        in_specs=[hbm] * 3,
        out_specs=(vmem,) * 6,
        scratch_shapes=[
            pltpu.VMEM((TIERS, BAND, COLS), f32),
            pltpu.VMEM((TIERS, BAND, COLS), f32),
            pltpu.VMEM((BAND, COLS), i32),
            pltpu.VMEM((2 * NX, BOX, LANES), f32),
            pltpu.VMEM((NX, ROWS, LANES), i32),
            pltpu.VMEM((NX, KEPT, LANES), i32),
            pltpu.VMEM((NX, ROWS, LANES), i32),
            pltpu.VMEM((NX, ROWS, LANES), i32),
            pltpu.VMEM((NX, BAND, LANES), f32),
            pltpu.VMEM((NX, BAND, LANES), f32),
            pltpu.VMEM((NX, BAND, LANES), f32),
            pltpu.VMEM((2, BAND, LANES), f32),
            pltpu.VMEM((2, 24, CI), f32),
            pltpu.VMEM((2, 24, CI), f32),
            pltpu.SemaphoreType.DMA((2 * CHUNKS + 1,)),
            pltpu.SemaphoreType.DMA((CHUNKS, NX)),
            pltpu.SemaphoreType.DMA((CHUNKS, NX)),
            pltpu.SemaphoreType.DMA((NX,)),
            pltpu.SemaphoreType.DMA((NX,)),
            pltpu.SemaphoreType.DMA((NX,)),
            pltpu.SemaphoreType.DMA((2,)),
            pltpu.SemaphoreType.DMA((2,)),
            pltpu.SemaphoreType.DMA((2,)),
        ],
        compiler_params=pltpu.CompilerParams(collective_id=0, has_side_effects=True, vmem_limit_bytes=48 * 2**20),
        name="exchange",
    )(warmth, salt, tally)
    return pl.pallas_call(
        finish,
        out_shape=(jax.ShapeDtypeStruct((TIERS, CJ, CI), f32),) * 2,
        in_specs=[vmem] * 6,
        out_specs=(hbm,) * 2,
        scratch_shapes=[
            pltpu.VMEM((2, TIERS, BAND, CI), f32),
            pltpu.VMEM((TIERS - EARLY, CJ - 2 * BAND, CI), f32),
            pltpu.SemaphoreType.DMA((6,)),
        ],
        compiler_params=pltpu.CompilerParams(vmem_limit_bytes=16 * 2**20),
        name="finish",
    )(*held)


def solution(mesh):
    placed = (P(None, ("ty", "tx"), None), P(None, ("ty", "tx"), None), P(("ty", "tx"), None))
    return jax.shard_map(
        on_device,
        mesh=mesh,
        in_specs=placed,
        out_specs=(P(None, "ty", "tx"), P(None, "ty", "tx")),
        check_vma=False,
    )
```

time: 66.6 us -> 58.7 us (0.88)
  Pallas kernels: 64.9 us -> 57.1 us
    pallas_call x2, Pallas kernels: 64.9 us -> 57.1 us  [the longest x1 53.6 us: on_device(): pl.pallas_call(exchange, out_shape=(pltpu.VMEM((TIERS, CJ, CI), f32), plt...]
where the time goes in v2:
time: 58.7 us; the launch traced here: 57.7 us
  Pallas kernels  57.1 us (97%)
  between operations  0.64 us (1%)
    pallas_call x1, Pallas kernels, on_device(): pl.pallas_call(exchange, out_shape=(pltpu.VMEM((TIERS, CJ, CI), f32), plt...  53.6 us
    pallas_call x1, Pallas kernels, on_device(): pl.pallas_call(finish, out_shape=(jax.ShapeDtypeStruct((TIERS, CJ, CI), f...  3.49 us

profile of v2, /device:TPU:7, one launch (start us, length us, event | category | flops | bytes accessed | tf_op | source)
XLA Modules:
  0.0 57.7 jit_solution(8187521769400428271)
XLA Ops:
  0.6 53.6 %exchange.1 = (f32[16,128,512]{2,1,0:T(8,128)S(1)}, f32[16,128,512]{2,1,0:T(8,128)S(1)}, f32[128,512]{1,0:T(8,128)S(1)}, f32[4,128,512]{2,1,0:T(8,128)S(1)}, f32...) custom-call(f32[16,8,8192]{2,1,0:T(8,128)} %warmth.1, f32[16,8,8192]{2,1,0:T(8,128)} %salt.1, s32[8,8192]{1,0:T(8,128)} %tally.1), custom_call_target="tpu_custom_call" | custom-call | tf_op jit(solution)/shard_map/exchange/pallas_call | solution.py:471
  54.3 3.5 %finish.1 = (f32[16,128,512]{2,1,0:T(8,128)}, f32[16,128,512]{2,1,0:T(8,128)}) custom-call(f32[16,128,512]{2,1,0:T(8,128)S(1)} %get-tuple-element.8.field, f32[16,128,512]{2,1,0:T(8,128)S(1)} %get-tuple-element.9.lap, f32[128,512]{1,0:T(8,128)S(1)} %get-tuple-element.10.depth, f32[4,128,512]{2,1,0:T(8,128)S(1)} %get-tuple-element.11.least, ...), custom_call_target="tpu_custom_call" | custom-call | tf_op jit(solution)/shard_map/finish/pallas_call | solution.py:511

commit v3 on v2

--- a/solution.py
+++ b/solution.py
@@ -31,7 +31,7 @@
 BOX = ROWS + TIERS * KEPT
 INNER = range(1, NX - 1)
 LAST = NX - 1
-FAR = ((2, 2), (2, 1), (2, 3), (1, 2), (3, 2), (1, 1), (3, 3), (1, 3), (3, 1), (2, 0), (0, 2), (1, 0), (3, 0), (0, 1), (0, 3), (0, 0))
+FAR = ((0, 2), (2, 2), (0, 1), (1, 1), (3, 3), (0, 3), (2, 1), (2, 3), (1, 2), (3, 2), (1, 3), (3, 1), (2, 0), (1, 0), (3, 0), (0, 0))
 f32 = jnp.float32
 i32 = jnp.int32
 
@@ -172,6 +172,7 @@
         part = pl.ds(CUTS[chunk], CUTS[chunk + 1] - CUTS[chunk])
         loads.append(pltpu.make_async_copy(warmth.at[part], heat.at[part], in_sem.at[2 * chunk]))
         loads.append(pltpu.make_async_copy(salt.at[part], brine.at[part], in_sem.at[2 * chunk + 1]))
+    loads[0].start()
     for step in range(1, NX):
         pl.semaphore_signal(barrier, inc=1, device_id={"tx": (tx + step) & LAST}, device_id_type=MESH)
 
@@ -183,14 +184,15 @@
     def _():
         pl.semaphore_signal(barrier, inc=1, device_id={"ty": ty + 1}, device_id_type=MESH)
 
-    for load in loads:
+    for load in loads[1:]:
         load.start()
     lanes = lax.broadcasted_iota(i32, (BAND, LANES), 1)
     partners = [((tx // 4 + dy) & 3) * 4 + ((tx + dz) & 3) for dy, dz in FAR[:-1]]
 
     def box_copy(chunk, to, source):
-        low = 0 if chunk == 0 else ROWS + KEPT * CUTS[chunk]
-        part = pl.ds(low, ROWS + KEPT * CUTS[chunk + 1] - low)
+        part = pl.ds(0, ROWS)
+        if chunk < CHUNKS:
+            part = pl.ds(ROWS + KEPT * CUTS[chunk], KEPT * (CUTS[chunk + 1] - CUTS[chunk]))
         return pltpu.make_async_remote_copy(
             src_ref=boxes.at[to, part], dst_ref=boxes.at[NX + source, part],
             send_sem=send_sem.at[chunk, to], recv_sem=recv_sem.at[chunk, source],
@@ -211,6 +213,18 @@
             send_sem=brink_ssem.at[to], recv_sem=brink_rsem.at[side],
             device_id={"tx": to}, device_id_type=MESH,
         )
+
+    def find(to):
+        at = pl.ds(pl.multiple_of(to * CI, CI), CI)
+        deep = bottom[:, at]
+        lane_from, row_from = packing(as_rows(deep), pltpu.roll)
+        pack_lane[to] = lane_from
+        pack_row[to] = row_from
+        deep = deep.astype(f32)
+        low = pltpu.roll(deep[:, CI - LANES :], TIERS + 1, 1)
+        high = pltpu.roll(deep[:, :LANES], 32 + TIERS, 1)
+        rim_low[(to + 1) & LAST] = jnp.where(lanes == TIERS, low, 0.0)
+        rim_high[(to + LAST) & LAST] = jnp.where(lanes == 32 + TIERS, high, 0.0)
 
     def make(first, last, step):
         to = partner_of(tx, step)
@@ -220,18 +234,8 @@
         at = pl.ds(pl.multiple_of(to * CI, CI), CI)
         low = jnp.zeros((BAND, LANES), f32)
         high = jnp.zeros((BAND, LANES), f32)
-        if first == 0:
-            deep = bottom[:, at]
-            lane_from, row_from = packing(as_rows(deep), pltpu.roll)
-            pack_lane[to] = lane_from
-            pack_row[to] = row_from
-            deep = deep.astype(f32)
-            boxes[slot, :ROWS] = as_rows(deep)
-            low = jnp.where(lanes == TIERS, pltpu.roll(deep[:, CI - LANES :], TIERS + 1, 1), low)
-            high = jnp.where(lanes == 32 + TIERS, pltpu.roll(deep[:, :LANES], 32 + TIERS, 1), high)
-        else:
-            lane_from = pack_lane[to]
-            row_from = pack_row[to]
+        lane_from = pack_lane[to]
+        row_from = pack_row[to]
         for tier in range(first, last):
             value = density(heat[tier, :, at], brine[tier, :, at], tier)
             boxes[slot, ROWS + KEPT * tier : ROWS + KEPT * tier + KEPT] = pack(as_rows(value), lane_from, row_from)
@@ -242,10 +246,11 @@
                 for v in range(CI // LANES):
                     place = (tier - EARLY) * (CI // LANES) + v
                     brink_out[to, place : place + 1] = brink[:, LANES * v : LANES * v + LANES]
-        if first == 0:
-            rim_low[east] = low
-            rim_high[west] = high
-        else:
+        return east, low, west, high
+
+    def make_two(first, last, pair):
+        rims_of = [make(first, last, 2 * pair + n) for n in (0, 1)]
+        for east, low, west, high in rims_of:
             rim_low[east] = rim_low[east] + low
             rim_high[west] = rim_high[west] + high
 
@@ -253,38 +258,49 @@
         loads[1 + 2 * chunk].wait()
         loads[2 + 2 * chunk].wait()
 
-    def make_only(first, last):
-        def one(step, carry):
-            make(first, last, step)
+    def make_and_send(first, last, sends, before):
+        def one(pair, carry):
+            make_two(first, last, pair)
+
+            @pl.when(pair > 0)
+            def _():
+                if sends is not None:
+                    box_copy(sends, partner_of(tx, 2 * pair - 2), tx).start()
+                    box_copy(sends, partner_of(tx, 2 * pair - 1), tx).start()
+
+            @pl.when(pair == 0)
+            def _():
+                if before is not None:
+                    box_copy(before, partners[LAST - 1], tx).start()
+
             return carry
 
-        return one
-
-    def make_and_send(chunk):
-        def one(step, carry):
-            make(CUTS[chunk], CUTS[chunk + 1], step)
-
-            @pl.when(step > 0)
-            def _():
-                box_copy(chunk, partner_of(tx, step - 1), tx).start()
-
-            return carry
-
-        return one
+        lax.fori_loop(0, NX // 2, one, 0)
+
+    def find_four(four, carry):
+        for n in range(4):
+            find(4 * four + n)
+        return carry
+
+    def take_tally(to, carry):
+        at = pl.ds(pl.multiple_of(to * CI, CI), CI)
+        boxes[jnp.where(to == tx, NX + to, to), :ROWS] = as_rows(bottom[:, at]).astype(f32)
+        return carry
 
     loads[0].wait()
-    wait_loads(0)
-    lax.fori_loop(0, 3, make_only(CUTS[0], CUTS[1]), 0)
+    lax.fori_loop(0, NX, take_tally, 0, unroll=4)
     neighbours = jnp.where(ty > 0, 1, 0) + jnp.where(ty < NY - 1, 1, 0)
     pl.semaphore_wait(barrier, NX - 1 + neighbours)
-    for to in partners[:2]:
-        box_copy(0, to, tx).start()
-    lax.fori_loop(3, NX, make_and_send(0), 0)
+    for to in partners:
+        box_copy(CHUNKS, to, tx).start()
+    lax.fori_loop(0, NX // 4, find_four, 0)
+    wait_loads(0)
+    make_and_send(CUTS[0], CUTS[1], 0, None)
     wait_loads(1)
-    lax.fori_loop(0, NX, make_and_send(1), 0)
+    make_and_send(CUTS[1], CUTS[2], 1, 0)
     wait_loads(2)
     wait_loads(3)
-    lax.fori_loop(0, NX, make_only(CUTS[2], CUTS[4]), 0)
+    make_and_send(CUTS[2], CUTS[4], None, 1)
 
     def join(to, carry):
         rim_low[to] = rim_low[to] + rim_high[to]
@@ -308,6 +324,8 @@
     def arrive(chunk, source):
         @pl.when(source != tx)
         def _():
+            if chunk == 0:
+                box_copy(CHUNKS, source, source).wait_recv()
             box_copy(chunk, source, source).wait_recv()
 
         rows = pl.ds(pl.multiple_of(source * BAND, BAND), BAND)
@@ -402,6 +420,16 @@
 
     arrive_all(2, 2, LAST)
     laplace(2)
+
+    @pl.when(outer)
+    def _():
+        for to in partners:
+            brink_copy(to, tx).wait_send()
+
+    for to in partners:
+        rim_copy(to, tx).wait_send()
+        for chunk in (CHUNKS, 0, 1, 2):
+            box_copy(chunk, to, tx).wait_send()
     arrive_all(3)
 
     @pl.when(ty > 0)
@@ -425,15 +453,8 @@
     flipped = [jnp.take_along_axis(upper[:, LANES * v : LANES * v + LANES], turn, axis=1) for v in (3, 2, 1, 0)]
     edges[1] = jnp.where(ty == NY - 1, jnp.concatenate(flipped, axis=1), upper)
 
-    @pl.when(outer)
-    def _():
-        for to in partners:
-            brink_copy(to, tx).wait_send()
-
     for to in partners:
-        rim_copy(to, tx).wait_send()
-        for chunk in range(CHUNKS):
-            box_copy(chunk, to, tx).wait_send()
+        box_copy(3, to, tx).wait_send()
 
 
 def finish(field, lap, depth, least, rims, edges, field_out, lap_out, ends, late, sem):
@@ -496,8 +517,8 @@
             pltpu.VMEM((2, 24, CI), f32),
             pltpu.VMEM((2, 24, CI), f32),
             pltpu.SemaphoreType.DMA((2 * CHUNKS + 1,)),
-            pltpu.SemaphoreType.DMA((CHUNKS, NX)),
-            pltpu.SemaphoreType.DMA((CHUNKS, NX)),
+            pltpu.SemaphoreType.DMA((CHUNKS + 1, NX)),
+            pltpu.SemaphoreType.DMA((CHUNKS + 1, NX)),
             pltpu.SemaphoreType.DMA((NX,)),
             pltpu.SemaphoreType.DMA((NX,)),
             pltpu.SemaphoreType.DMA((NX,)),

time: 58.7 us -> 55.9 us (0.952)
  Pallas kernels: 57.1 us -> 54.4 us
    pallas_call x1, Pallas kernels: 53.6 us -> 50.9 us  [on_device(): pl.pallas_call(exchange, out_shape=(pltpu.VMEM((TIERS, CJ, CI), f32), plt...]
where the time goes in v3:
time: 55.9 us; the launch traced here: 55 us
  Pallas kernels  54.4 us (97%)
  between operations  0.64 us (1%)
    pallas_call x1, Pallas kernels, on_device(): pl.pallas_call(exchange, out_shape=(pltpu.VMEM((TIERS, CJ, CI), f32), plt...  50.9 us
    pallas_call x1, Pallas kernels, on_device(): pl.pallas_call(finish, out_shape=(jax.ShapeDtypeStruct((TIERS, CJ, CI), f...  3.49 us

profile of v3, /device:TPU:7, one launch (start us, length us, event | category | flops | bytes accessed | tf_op | source)
XLA Modules:
  0.0 55.0 jit_solution(1699833541596976346)
XLA Ops:
  0.6 50.9 %exchange.1 = (f32[16,128,512]{2,1,0:T(8,128)S(1)}, f32[16,128,512]{2,1,0:T(8,128)S(1)}, f32[128,512]{1,0:T(8,128)S(1)}, f32[4,128,512]{2,1,0:T(8,128)S(1)}, f32...) custom-call(f32[16,8,8192]{2,1,0:T(8,128)} %warmth.1, f32[16,8,8192]{2,1,0:T(8,128)} %salt.1, s32[8,8192]{1,0:T(8,128)} %tally.1), custom_call_target="tpu_custom_call" | custom-call | tf_op jit(solution)/shard_map/exchange/pallas_call | solution.py:492
  51.6 3.5 %finish.1 = (f32[16,128,512]{2,1,0:T(8,128)}, f32[16,128,512]{2,1,0:T(8,128)}) custom-call(f32[16,128,512]{2,1,0:T(8,128)S(1)} %get-tuple-element.8.field, f32[16,128,512]{2,1,0:T(8,128)S(1)} %get-tuple-element.9.lap, f32[128,512]{1,0:T(8,128)S(1)} %get-tuple-element.10.depth, f32[4,128,512]{2,1,0:T(8,128)S(1)} %get-tuple-element.11.least, ...), custom_call_target="tpu_custom_call" | custom-call | tf_op jit(solution)/shard_map/finish/pallas_call | solution.py:532

commit v4 on v3

--- a/solution.py
+++ b/solution.py
@@ -28,7 +28,9 @@
 CUTS = (0, 5, 10, 14, 16)
 CHUNKS = len(CUTS) - 1
 EARLY = CUTS[-2]
-BOX = ROWS + TIERS * KEPT
+DONE = CUTS[-3]
+RIM = ROWS + CUTS[1] * KEPT
+BOX = ROWS + TIERS * KEPT + BAND
 INNER = range(1, NX - 1)
 LAST = NX - 1
 FAR = ((0, 2), (2, 2), (0, 1), (1, 1), (3, 3), (0, 3), (2, 1), (2, 3), (1, 2), (3, 2), (1, 3), (3, 1), (2, 0), (1, 0), (3, 0), (0, 0))
@@ -45,13 +47,17 @@
     return heat * a + salty * b
 
 
-def partner_of(tx, step):
+def partner_of(tx, step, way=1):
     dy = jnp.int32(0)
     dz = jnp.int32(0)
     for number, (far_y, far_z) in enumerate(FAR):
         dy = jnp.where(step == number, far_y, dy)
         dz = jnp.where(step == number, far_z, dz)
-    return ((tx // 4 + dy) & 3) * 4 + ((tx + dz) & 3)
+    return ((tx // 4 + way * dy) & 3) * 4 + ((tx + way * dz) & 3)
+
+
+def row_of(tier):
+    return ROWS + KEPT * tier + (BAND if tier >= CUTS[1] else 0)
 
 
 def as_rows(block):
@@ -160,8 +166,8 @@
 
 def exchange(
     warmth, salt, tally, out, lap, depth, least, rims, edges,
-    heat, brine, bottom, boxes, pack_lane, pack_row, lane_back, row_back, rim_low, rim_high, brink_out, brink_in, rows_out, rows_in,
-    in_sem, send_sem, recv_sem, rim_ssem, rim_rsem, brink_ssem, brink_rsem, row_ssem, row_rsem,
+    heat, brine, bottom, boxes, pack_lane, pack_row, lane_back, row_back, brink_out, brink_in, rows_out, rows_in,
+    in_sem, send_sem, recv_sem, brink_ssem, brink_rsem, row_ssem, row_rsem,
 ):
     ty = lax.axis_index("ty")
     tx = lax.axis_index("tx")
@@ -192,17 +198,11 @@
     def box_copy(chunk, to, source):
         part = pl.ds(0, ROWS)
         if chunk < CHUNKS:
-            part = pl.ds(ROWS + KEPT * CUTS[chunk], KEPT * (CUTS[chunk + 1] - CUTS[chunk]))
+            first = RIM if chunk == 1 else row_of(CUTS[chunk])
+            part = pl.ds(first, row_of(CUTS[chunk + 1] - 1) + KEPT - first)
         return pltpu.make_async_remote_copy(
             src_ref=boxes.at[to, part], dst_ref=boxes.at[NX + source, part],
             send_sem=send_sem.at[chunk, to], recv_sem=recv_sem.at[chunk, source],
-            device_id={"tx": to}, device_id_type=MESH,
-        )
-
-    def rim_copy(to, source):
-        return pltpu.make_async_remote_copy(
-            src_ref=rim_low.at[to], dst_ref=rims.at[source],
-            send_sem=rim_ssem.at[to], recv_sem=rim_rsem.at[source],
             device_id={"tx": to}, device_id_type=MESH,
         )
 
@@ -216,43 +216,40 @@
 
     def find(to):
         at = pl.ds(pl.multiple_of(to * CI, CI), CI)
-        deep = bottom[:, at]
-        lane_from, row_from = packing(as_rows(deep), pltpu.roll)
+        lane_from, row_from = packing(as_rows(bottom[:, at]), pltpu.roll)
         pack_lane[to] = lane_from
         pack_row[to] = row_from
-        deep = deep.astype(f32)
-        low = pltpu.roll(deep[:, CI - LANES :], TIERS + 1, 1)
-        high = pltpu.roll(deep[:, :LANES], 32 + TIERS, 1)
-        rim_low[(to + 1) & LAST] = jnp.where(lanes == TIERS, low, 0.0)
-        rim_high[(to + LAST) & LAST] = jnp.where(lanes == 32 + TIERS, high, 0.0)
+        return lane_from, row_from
+
+    def make_rim(to):
+        west = pl.ds(pl.multiple_of(((to * CI) + COLS - LANES) & (COLS - 1), LANES), LANES)
+        east = pl.ds(pl.multiple_of(((to * CI) + CI) & (COLS - 1), LANES), LANES)
+        rim = pltpu.roll(bottom[:, west].astype(f32), TIERS + 1, 1)
+        rim = jnp.where(lanes == 32 + TIERS, pltpu.roll(bottom[:, east].astype(f32), 32 + TIERS, 1), rim)
+        for tier in range(TIERS):
+            low = density(heat[tier, :, west], brine[tier, :, west], tier)
+            high = density(heat[tier, :, east], brine[tier, :, east], tier)
+            rim = jnp.where(lanes == tier, pltpu.roll(low, tier + 1, 1), rim)
+            rim = jnp.where(lanes == 32 + tier, pltpu.roll(high, 32 + tier, 1), rim)
+        boxes[jnp.where(to == tx, NX + to, to), RIM : RIM + BAND] = rim
 
     def make(first, last, step):
         to = partner_of(tx, step)
         slot = jnp.where(step == LAST, NX + to, to)
-        east = (to + 1) & LAST
-        west = (to + LAST) & LAST
         at = pl.ds(pl.multiple_of(to * CI, CI), CI)
-        low = jnp.zeros((BAND, LANES), f32)
-        high = jnp.zeros((BAND, LANES), f32)
-        lane_from = pack_lane[to]
-        row_from = pack_row[to]
+        lane_from, row_from = find(to) if first == 0 else (pack_lane[to], pack_row[to])
         for tier in range(first, last):
             value = density(heat[tier, :, at], brine[tier, :, at], tier)
-            boxes[slot, ROWS + KEPT * tier : ROWS + KEPT * tier + KEPT] = pack(as_rows(value), lane_from, row_from)
-            low = jnp.where(lanes == tier, pltpu.roll(value[:, CI - LANES :], tier + 1, 1), low)
-            high = jnp.where(lanes == 32 + tier, pltpu.roll(value[:, :LANES], 32 + tier, 1), high)
+            boxes[slot, row_of(tier) : row_of(tier) + KEPT] = pack(as_rows(value), lane_from, row_from)
             if tier >= EARLY:
                 brink = jnp.where(tx == 0, value[:1], value[BAND - 1 :])
                 for v in range(CI // LANES):
                     place = (tier - EARLY) * (CI // LANES) + v
                     brink_out[to, place : place + 1] = brink[:, LANES * v : LANES * v + LANES]
-        return east, low, west, high
 
     def make_two(first, last, pair):
-        rims_of = [make(first, last, 2 * pair + n) for n in (0, 1)]
-        for east, low, west, high in rims_of:
-            rim_low[east] = rim_low[east] + low
-            rim_high[west] = rim_high[west] + high
+        for n in (0, 1):
+            make(first, last, 2 * pair + n)
 
     def wait_loads(chunk):
         loads[1 + 2 * chunk].wait()
@@ -276,11 +273,6 @@
             return carry
 
         lax.fori_loop(0, NX // 2, one, 0)
-
-    def find_four(four, carry):
-        for n in range(4):
-            find(4 * four + n)
-        return carry
 
     def take_tally(to, carry):
         at = pl.ds(pl.multiple_of(to * CI, CI), CI)
@@ -293,21 +285,20 @@
     pl.semaphore_wait(barrier, NX - 1 + neighbours)
     for to in partners:
         box_copy(CHUNKS, to, tx).start()
-    lax.fori_loop(0, NX // 4, find_four, 0)
     wait_loads(0)
     make_and_send(CUTS[0], CUTS[1], 0, None)
-    wait_loads(1)
-    make_and_send(CUTS[1], CUTS[2], 1, 0)
-    wait_loads(2)
-    wait_loads(3)
+    for chunk in range(1, CHUNKS):
+        wait_loads(chunk)
+
+    def rim_two(pair, carry):
+        make_rim(2 * pair)
+        make_rim(2 * pair + 1)
+        return carry
+
+    lax.fori_loop(0, NX // 2, rim_two, 0)
+    box_copy(0, partners[LAST - 1], tx).start()
+    make_and_send(CUTS[1], CUTS[2], 1, None)
     make_and_send(CUTS[2], CUTS[4], None, 1)
-
-    def join(to, carry):
-        rim_low[to] = rim_low[to] + rim_high[to]
-        return carry
-
-    lax.fori_loop(0, NX, join, 0)
-    rims[tx] = rim_low[tx]
 
     @pl.when(outer)
     def _():
@@ -315,8 +306,6 @@
         for to in partners:
             brink_copy(to, tx).start()
 
-    for to in partners:
-        rim_copy(to, tx).start()
     for chunk in (2, 3):
         for to in partners:
             box_copy(chunk, to, tx).start()
@@ -340,16 +329,18 @@
             row_from = row_back[source]
             lane_from = lane_back[source]
             deep = as_block(deep)
+        if chunk == 1:
+            rims[source] = boxes[NX + source, RIM : RIM + BAND]
         for tier in range(CUTS[chunk], CUTS[chunk + 1]):
-            kept = boxes[NX + source, ROWS + KEPT * tier : ROWS + KEPT * tier + KEPT]
+            kept = boxes[NX + source, row_of(tier) : row_of(tier) + KEPT]
             out[tier, rows] = jnp.where(deep > tier, as_block(unpack(kept, row_from, lane_from)), 0.0)
 
-    def arrive_all(chunk, first=0, last=NX):
-        def one(source, carry):
-            arrive(chunk, source)
+    def arrive_all(chunk):
+        def one(step, carry):
+            arrive(chunk, partner_of(tx, (step + LAST) & LAST, -1))
             return carry
 
-        lax.fori_loop(first, last, one, 0)
+        lax.fori_loop(0, NX, one, 0)
 
     def laplace(chunk):
         def one(tier, carry):
@@ -364,14 +355,6 @@
     arrive_all(0)
     arrive_all(1)
 
-    def rim_in(source, carry):
-        @pl.when(source != tx)
-        def _():
-            rim_copy(source, source).wait_recv()
-
-        return carry
-
-    lax.fori_loop(0, NX, rim_in, 0)
     for band in INNER:
         here, *others = around(depth, band, TIERS, rims)
         for side, other in enumerate(others):
@@ -379,8 +362,7 @@
     laplace(0)
     laplace(1)
 
-    arrive(2, 0)
-    arrive(2, LAST)
+    arrive_all(2)
     for side, at in ((0, 0), (1, CJ - 1)):
         @pl.when(tx != (LAST if side else 0))
         def _():
@@ -392,8 +374,6 @@
         for place in range((TIERS - EARLY) * CI // LANES):
             tier, v = EARLY + place // (CI // LANES), place % (CI // LANES)
             rows_out[side, tier : tier + 1, LANES * v : LANES * v + LANES] = brink_in[side, place : place + 1]
-
-    arrive(2, 1)
 
     def row_copy(side, along):
         place = 1 - side if along == "ty" else 1
@@ -406,30 +386,29 @@
             device_id=device, device_id_type=MESH,
         )
 
-    @pl.when(ty > 0)
-    def _():
-        row_copy(0, "ty").start()
-
-    @pl.when(ty < NY - 1)
-    def _():
-        row_copy(1, "ty").start()
-
-    @pl.when(ty == NY - 1)
-    def _():
-        row_copy(1, "tx").start()
-
-    arrive_all(2, 2, LAST)
-    laplace(2)
-
     @pl.when(outer)
     def _():
         for to in partners:
             brink_copy(to, tx).wait_send()
 
     for to in partners:
-        rim_copy(to, tx).wait_send()
-        for chunk in (CHUNKS, 0, 1, 2):
+        for chunk in (CHUNKS, 0, 1):
             box_copy(chunk, to, tx).wait_send()
+
+    @pl.when(ty > 0)
+    def _():
+        row_copy(0, "ty").start()
+
+    @pl.when(ty < NY - 1)
+    def _():
+        row_copy(1, "ty").start()
+
+    @pl.when(ty == NY - 1)
+    def _():
+        row_copy(1, "tx").start()
+
+    for to in partners:
+        box_copy(2, to, tx).wait_send()
     arrive_all(3)
 
     @pl.when(ty > 0)
@@ -461,7 +440,7 @@
     middle = pl.ds(BAND, CJ - 2 * BAND)
     half = TIERS // 2
     copies = [pltpu.make_async_copy(field.at[pl.ds(half * n, half)], field_out.at[pl.ds(half * n, half)], sem.at[n]) for n in (0, 1)]
-    copies.append(pltpu.make_async_copy(lap.at[pl.ds(0, EARLY), middle], lap_out.at[pl.ds(0, EARLY), middle], sem.at[2]))
+    copies.append(pltpu.make_async_copy(lap.at[pl.ds(0, DONE), middle], lap_out.at[pl.ds(0, DONE), middle], sem.at[2]))
     for copy in copies:
         copy.start()
 
@@ -476,12 +455,14 @@
             ends[place, tier] = divergence(outer(field.at[tier], tier, band), bounds, tier)
         copies.append(pltpu.make_async_copy(ends.at[place], lap_out.at[:, pl.ds(BAND * band, BAND)], sem.at[3 + place]))
         copies[-1].start()
-    for tier in range(EARLY, TIERS):
-        for band in INNER:
-            bounds = [least[side, BAND * band : BAND * band + BAND] for side in range(4)]
-            late[tier - EARLY, BAND * (band - 1) : BAND * band] = divergence(around(field.at[tier], band, tier, rims), bounds, tier)
-    copies.append(pltpu.make_async_copy(late, lap_out.at[pl.ds(EARLY, TIERS - EARLY), middle], sem.at[5]))
-    copies[-1].start()
+    for part in range((TIERS - DONE) // 2):
+        for tier in (DONE + 2 * part, DONE + 2 * part + 1):
+            for band in INNER:
+                bounds = [least[side, BAND * band : BAND * band + BAND] for side in range(4)]
+                late[tier - DONE, BAND * (band - 1) : BAND * band] = divergence(around(field.at[tier], band, tier, rims), bounds, tier)
+        two = pl.ds(DONE + 2 * part, 2)
+        copies.append(pltpu.make_async_copy(late.at[pl.ds(2 * part, 2)], lap_out.at[two, middle], sem.at[5 + part]))
+        copies[-1].start()
     for copy in copies:
         copy.wait()
 
@@ -511,16 +492,12 @@
             pltpu.VMEM((NX, ROWS, LANES), i32),
             pltpu.VMEM((NX, ROWS, LANES), i32),
             pltpu.VMEM((NX, BAND, LANES), f32),
-            pltpu.VMEM((NX, BAND, LANES), f32),
-            pltpu.VMEM((NX, BAND, LANES), f32),
             pltpu.VMEM((2, BAND, LANES), f32),
             pltpu.VMEM((2, 24, CI), f32),
             pltpu.VMEM((2, 24, CI), f32),
             pltpu.SemaphoreType.DMA((2 * CHUNKS + 1,)),
             pltpu.SemaphoreType.DMA((CHUNKS + 1, NX)),
             pltpu.SemaphoreType.DMA((CHUNKS + 1, NX)),
-            pltpu.SemaphoreType.DMA((NX,)),
-            pltpu.SemaphoreType.DMA((NX,)),
             pltpu.SemaphoreType.DMA((NX,)),
             pltpu.SemaphoreType.DMA((2,)),
             pltpu.SemaphoreType.DMA((2,)),
@@ -536,8 +513,8 @@
         out_specs=(hbm,) * 2,
         scratch_shapes=[
             pltpu.VMEM((2, TIERS, BAND, CI), f32),
-            pltpu.VMEM((TIERS - EARLY, CJ - 2 * BAND, CI), f32),
-            pltpu.SemaphoreType.DMA((6,)),
+            pltpu.VMEM((TIERS - DONE, CJ - 2 * BAND, CI), f32),
+            pltpu.SemaphoreType.DMA((5 + (TIERS - DONE) // 2,)),
         ],
         compiler_params=pltpu.CompilerParams(vmem_limit_bytes=16 * 2**20),
         name="finish",

time: 55.9 us -> 54.3 us (0.971); the launches traced: 55 us -> 54.2 us
  Pallas kernels: 54.4 us -> 53.6 us
    pallas_call x1, Pallas kernels: 50.9 us -> 50 us  [on_device(): pl.pallas_call(exchange, out_shape=(pltpu.VMEM((TIERS, CJ, CI), f32), plt...]
where the time goes in v4:
time: 54.3 us; the launch traced here: 54.2 us
  Pallas kernels  53.6 us (99%)
  between operations  0.64 us (1%)
    pallas_call x1, Pallas kernels, on_device(): pl.pallas_call(exchange, out_shape=(pltpu.VMEM((TIERS, CJ, CI), f32), plt...  50 us
    pallas_call x1, Pallas kernels, on_device(): pl.pallas_call(finish, out_shape=(jax.ShapeDtypeStruct((TIERS, CJ, CI), f...  3.51 us

profile of v4, /device:TPU:7, one launch (start us, length us, event | category | flops | bytes accessed | tf_op | source)
XLA Modules:
  0.0 54.2 jit_solution(11771155549400428203)
XLA Ops:
  0.6 50.0 %exchange.1 = (f32[16,128,512]{2,1,0:T(8,128)S(1)}, f32[16,128,512]{2,1,0:T(8,128)S(1)}, f32[128,512]{1,0:T(8,128)S(1)}, f32[4,128,512]{2,1,0:T(8,128)S(1)}, f32...) custom-call(f32[16,8,8192]{2,1,0:T(8,128)} %warmth.1, f32[16,8,8192]{2,1,0:T(8,128)} %salt.1, s32[8,8192]{1,0:T(8,128)} %tally.1), custom_call_target="tpu_custom_call" | custom-call | tf_op jit(solution)/shard_map/exchange/pallas_call | solution.py:473
  50.7 3.5 %finish.1 = (f32[16,128,512]{2,1,0:T(8,128)}, f32[16,128,512]{2,1,0:T(8,128)}) custom-call(f32[16,128,512]{2,1,0:T(8,128)S(1)} %get-tuple-element.8.field, f32[16,128,512]{2,1,0:T(8,128)S(1)} %get-tuple-element.9.lap, f32[128,512]{1,0:T(8,128)S(1)} %get-tuple-element.10.depth, f32[4,128,512]{2,1,0:T(8,128)S(1)} %get-tuple-element.11.least, ...), custom_call_target="tpu_custom_call" | custom-call | tf_op jit(solution)/shard_map/finish/pallas_call | solution.py:509

commit v5 on v4

--- a/solution.py
+++ b/solution.py
@@ -25,7 +25,7 @@
 ROWS = BAND * CI // LANES
 KEPT = 24
 SPARE = (ROWS - KEPT) * LANES
-CUTS = (0, 5, 10, 14, 16)
+CUTS = (0, 6, 10, 14, 16)
 CHUNKS = len(CUTS) - 1
 EARLY = CUTS[-2]
 DONE = CUTS[-3]
@@ -33,7 +33,9 @@
 BOX = ROWS + TIERS * KEPT + BAND
 INNER = range(1, NX - 1)
 LAST = NX - 1
-FAR = ((0, 2), (2, 2), (0, 1), (1, 1), (3, 3), (0, 3), (2, 1), (2, 3), (1, 2), (3, 2), (1, 3), (3, 1), (2, 0), (1, 0), (3, 0), (0, 0))
+ZFIRST = ((0, 2), (2, 2), (0, 1), (1, 1), (3, 3), (0, 3), (2, 1), (2, 3), (1, 2), (3, 2), (1, 3), (3, 1), (2, 0), (1, 0), (3, 0), (0, 0))
+FARFIRST = ((2, 2), (2, 1), (2, 3), (1, 2), (3, 2), (1, 1), (3, 3), (1, 3), (3, 1), (2, 0), (0, 2), (1, 0), (3, 0), (0, 1), (0, 3), (0, 0))
+ORDERS = (ZFIRST, FARFIRST, FARFIRST, FARFIRST, ZFIRST)
 f32 = jnp.float32
 i32 = jnp.int32
 
@@ -47,10 +49,10 @@
     return heat * a + salty * b
 
 
-def partner_of(tx, step, way=1):
+def partner_of(tx, step, chunk, way=1):
     dy = jnp.int32(0)
     dz = jnp.int32(0)
-    for number, (far_y, far_z) in enumerate(FAR):
+    for number, (far_y, far_z) in enumerate(ORDERS[chunk]):
         dy = jnp.where(step == number, far_y, dy)
         dz = jnp.where(step == number, far_z, dz)
     return ((tx // 4 + way * dy) & 3) * 4 + ((tx + way * dz) & 3)
@@ -193,7 +195,7 @@
     for load in loads[1:]:
         load.start()
     lanes = lax.broadcasted_iota(i32, (BAND, LANES), 1)
-    partners = [((tx // 4 + dy) & 3) * 4 + ((tx + dz) & 3) for dy, dz in FAR[:-1]]
+    partners = [[((tx // 4 + dy) & 3) * 4 + ((tx + dz) & 3) for dy, dz in order[:-1]] for order in ORDERS]
 
     def box_copy(chunk, to, source):
         part = pl.ds(0, ROWS)
@@ -234,7 +236,7 @@
         boxes[jnp.where(to == tx, NX + to, to), RIM : RIM + BAND] = rim
 
     def make(first, last, step):
-        to = partner_of(tx, step)
+        to = partner_of(tx, step, CUTS.index(first))
         slot = jnp.where(step == LAST, NX + to, to)
         at = pl.ds(pl.multiple_of(to * CI, CI), CI)
         lane_from, row_from = find(to) if first == 0 else (pack_lane[to], pack_row[to])
@@ -262,13 +264,13 @@
             @pl.when(pair > 0)
             def _():
                 if sends is not None:
-                    box_copy(sends, partner_of(tx, 2 * pair - 2), tx).start()
-                    box_copy(sends, partner_of(tx, 2 * pair - 1), tx).start()
+                    box_copy(sends, partner_of(tx, 2 * pair - 2, sends), tx).start()
+                    box_copy(sends, partner_of(tx, 2 * pair - 1, sends), tx).start()
 
             @pl.when(pair == 0)
             def _():
                 if before is not None:
-                    box_copy(before, partners[LAST - 1], tx).start()
+                    box_copy(before, partners[before][LAST - 1], tx).start()
 
             return carry
 
@@ -283,7 +285,7 @@
     lax.fori_loop(0, NX, take_tally, 0, unroll=4)
     neighbours = jnp.where(ty > 0, 1, 0) + jnp.where(ty < NY - 1, 1, 0)
     pl.semaphore_wait(barrier, NX - 1 + neighbours)
-    for to in partners:
+    for to in partners[CHUNKS]:
         box_copy(CHUNKS, to, tx).start()
     wait_loads(0)
     make_and_send(CUTS[0], CUTS[1], 0, None)
@@ -296,18 +298,18 @@
         return carry
 
     lax.fori_loop(0, NX // 2, rim_two, 0)
-    box_copy(0, partners[LAST - 1], tx).start()
+    box_copy(0, partners[0][LAST - 1], tx).start()
     make_and_send(CUTS[1], CUTS[2], 1, None)
     make_and_send(CUTS[2], CUTS[4], None, 1)
 
     @pl.when(outer)
     def _():
         brink_in[jnp.where(tx == 0, 0, 1)] = brink_out[tx]
-        for to in partners:
+        for to in partners[0]:
             brink_copy(to, tx).start()
 
     for chunk in (2, 3):
-        for to in partners:
+        for to in partners[chunk]:
             box_copy(chunk, to, tx).start()
 
     def arrive(chunk, source):
@@ -337,7 +339,7 @@
 
     def arrive_all(chunk):
         def one(step, carry):
-            arrive(chunk, partner_of(tx, (step + LAST) & LAST, -1))
+            arrive(chunk, partner_of(tx, (step + LAST) & LAST, chunk, -1))
             return carry
 
         lax.fori_loop(0, NX, one, 0)
@@ -388,10 +390,10 @@
 
     @pl.when(outer)
     def _():
-        for to in partners:
+        for to in partners[0]:
             brink_copy(to, tx).wait_send()
 
-    for to in partners:
+    for to in partners[0]:
         for chunk in (CHUNKS, 0, 1):
             box_copy(chunk, to, tx).wait_send()
 
@@ -407,7 +409,7 @@
     def _():
         row_copy(1, "tx").start()
 
-    for to in partners:
+    for to in partners[0]:
         box_copy(2, to, tx).wait_send()
     arrive_all(3)
 
@@ -432,7 +434,7 @@
     flipped = [jnp.take_along_axis(upper[:, LANES * v : LANES * v + LANES], turn, axis=1) for v in (3, 2, 1, 0)]
     edges[1] = jnp.where(ty == NY - 1, jnp.concatenate(flipped, axis=1), upper)
 
-    for to in partners:
+    for to in partners[0]:
         box_copy(3, to, tx).wait_send()
 
 

time: 54.3 us -> 53.8 us (level)
  no operation moved by 1% of the time
where the time goes in v5:
time: 53.8 us; the launch traced here: 53.7 us
  Pallas kernels  53.1 us (99%)
  between operations  0.64 us (1%)
    pallas_call x1, Pallas kernels, on_device(): pl.pallas_call(exchange, out_shape=(pltpu.VMEM((TIERS, CJ, CI), f32), plt...  49.5 us
    pallas_call x1, Pallas kernels, on_device(): pl.pallas_call(finish, out_shape=(jax.ShapeDtypeStruct((TIERS, CJ, CI), f...  3.51 us

profile of v5, /device:TPU:7, one launch (start us, length us, event | category | flops | bytes accessed | tf_op | source)
XLA Modules:
  0.0 53.7 jit_solution(14446398658854816049)
XLA Ops:
  0.6 49.5 %exchange.1 = (f32[16,128,512]{2,1,0:T(8,128)S(1)}, f32[16,128,512]{2,1,0:T(8,128)S(1)}, f32[128,512]{1,0:T(8,128)S(1)}, f32[4,128,512]{2,1,0:T(8,128)S(1)}, f32...) custom-call(f32[16,8,8192]{2,1,0:T(8,128)} %warmth.1, f32[16,8,8192]{2,1,0:T(8,128)} %salt.1, s32[8,8192]{1,0:T(8,128)} %tally.1), custom_call_target="tpu_custom_call" | custom-call | tf_op jit(solution)/shard_map/exchange/pallas_call | solution.py:475
  50.2 3.5 %finish.1 = (f32[16,128,512]{2,1,0:T(8,128)}, f32[16,128,512]{2,1,0:T(8,128)}) custom-call(f32[16,128,512]{2,1,0:T(8,128)S(1)} %get-tuple-element.8.field, f32[16,128,512]{2,1,0:T(8,128)S(1)} %get-tuple-element.9.lap, f32[128,512]{1,0:T(8,128)S(1)} %get-tuple-element.10.depth, f32[4,128,512]{2,1,0:T(8,128)S(1)} %get-tuple-element.11.least, ...), custom_call_target="tpu_custom_call" | custom-call | tf_op jit(solution)/shard_map/finish/pallas_call | solution.py:511

commit v6 on v5

--- a/solution.py
+++ b/solution.py
@@ -300,7 +300,8 @@
     lax.fori_loop(0, NX // 2, rim_two, 0)
     box_copy(0, partners[0][LAST - 1], tx).start()
     make_and_send(CUTS[1], CUTS[2], 1, None)
-    make_and_send(CUTS[2], CUTS[4], None, 1)
+    make_and_send(CUTS[2], CUTS[3], 2, 1)
+    make_and_send(CUTS[3], CUTS[4], None, 2)
 
     @pl.when(outer)
     def _():
@@ -308,9 +309,8 @@
         for to in partners[0]:
             brink_copy(to, tx).start()
 
-    for chunk in (2, 3):
-        for to in partners[chunk]:
-            box_copy(chunk, to, tx).start()
+    for to in partners[3]:
+        box_copy(3, to, tx).start()
 
     def arrive(chunk, source):
         @pl.when(source != tx)

time: 53.8 us -> 53.8 us (level)
  no operation moved by 1% of the time
where the time goes in v6:
time: 53.8 us; the launch traced here: 53.7 us
  Pallas kernels  53.1 us (99%)
  between operations  0.64 us (1%)
    pallas_call x1, Pallas kernels, on_device(): pl.pallas_call(exchange, out_shape=(pltpu.VMEM((TIERS, CJ, CI), f32), plt...  49.5 us
    pallas_call x1, Pallas kernels, on_device(): pl.pallas_call(finish, out_shape=(jax.ShapeDtypeStruct((TIERS, CJ, CI), f...  3.51 us

profile of v6, /device:TPU:7, one launch (start us, length us, event | category | flops | bytes accessed | tf_op | source)
XLA Modules:
  0.0 53.7 jit_solution(7582919331822290682)
XLA Ops:
  0.6 49.5 %exchange.1 = (f32[16,128,512]{2,1,0:T(8,128)S(1)}, f32[16,128,512]{2,1,0:T(8,128)S(1)}, f32[128,512]{1,0:T(8,128)S(1)}, f32[4,128,512]{2,1,0:T(8,128)S(1)}, f32...) custom-call(f32[16,8,8192]{2,1,0:T(8,128)} %warmth.1, f32[16,8,8192]{2,1,0:T(8,128)} %salt.1, s32[8,8192]{1,0:T(8,128)} %tally.1), custom_call_target="tpu_custom_call" | custom-call | tf_op jit(solution)/shard_map/exchange/pallas_call | solution.py:475
  50.2 3.5 %finish.1 = (f32[16,128,512]{2,1,0:T(8,128)}, f32[16,128,512]{2,1,0:T(8,128)}) custom-call(f32[16,128,512]{2,1,0:T(8,128)S(1)} %get-tuple-element.8.field, f32[16,128,512]{2,1,0:T(8,128)S(1)} %get-tuple-element.9.lap, f32[128,512]{1,0:T(8,128)S(1)} %get-tuple-element.10.depth, f32[4,128,512]{2,1,0:T(8,128)S(1)} %get-tuple-element.11.least, ...), custom_call_target="tpu_custom_call" | custom-call | tf_op jit(solution)/shard_map/finish/pallas_call | solution.py:511
